TPU v7x, 32 devices: a whole 2x2x4 slice. The times are simulated.
32 devices in a mesh: rep: 2 (over y), tile: 4 (over z), pen: 2 (over x), sub: 2 (over core).
Axes of the slice: x: 2, y: 2, z: 4, core: 2. Of those that a mesh axis runs over, the one named last changes fastest.
Arguments:
- positions: float32 [6, 4, 2, 512], P('rep', 'tile', 'pen'), parts along dimension 0, may hold values from 0 to 256, as said below
- velocities: float32 [6, 4, 2, 512], P('rep', 'tile', 'pen'), parts along dimension 0, may hold values from -5 to 5
- charges: float32 [8, 2, 512], P(('rep', 'tile'), 'pen'), parts along dimension 0, may hold values from -3 to 3
- inverse_mass: float32 [8, 2, 512], P(('rep', 'tile'), 'pen'), parts along dimension 0, may hold values from 0.06 to 1
- export_rows: int32 [8, 2, 128], P(('rep', 'tile'), 'pen'), parts along dimension 0, may hold values from 0 to 511, as said below
- partners: int32 [8, 2, 64, 512], P(('rep', 'tile'), 'pen', 'sub'), parts along dimension 0, may hold values from 0 to 1663, as said below
- bond_partners: int32 [8, 2, 4, 512], P(('rep', 'tile'), 'pen', 'sub'), parts along dimension 0, may hold values from 0 to 511, as said below
- bond_rest: float32 [8, 2, 4, 512], P(('rep', 'tile'), 'pen', 'sub'), parts along dimension 0, may hold values from 1 to 8
- block_offsets: int32 [6, 4, 2, 512], P('rep', 'tile', 'pen'), parts along dimension 0, may hold values from -1 to 254, as said below
Outputs:
- final_positions: float32 [6, 4, 2, 512], P('rep', 'tile', 'pen'), parts along dimension 0
- final_velocities: float32 [6, 4, 2, 512], P('rep', 'tile', 'pen'), parts along dimension 0
- potential: float32 [8, 2, 512], P(('rep', 'tile'), 'pen', 'sub'), parts along dimension 0
There are 2 independent parts, one for each index of `rep`. A program takes and returns all parts, laid end to end along the dimension named above; each array names one. Nothing has to cross between parts.
Inputs may be any that keep to these rules, and one draw needn't show every extreme that they name: `positions`: coordinates of an atom lie strictly between its block offset + 1 and its block offset + 2, coordinate by coordinate. `block_offsets`: for the patch (t, p), x offsets lie in t * 64 - 1 to t * 64 + 62 and y offsets in p * 128 - 1 to p * 128 + 126; z offsets lie in -1 to 254. `export_rows`: rows of the patch's own atoms. `partners`: columns of the patch's table; columns 1024 to 1151 are never named. Slots that an atom does not use name the atom itself. `bond_partners`: rows of the patch's own atoms.
All inputs are finite; a program needn't handle non-finite values.
Results may differ from a plain program's by a relative error of at most 0.0005.
Values sent between devices are 32-bit elements; how exact they have to be, the bound alone decides.
A program may use at most 128 MiB of HBM per device.

v0:
```python
import math

import jax
import jax.numpy as jnp
from jax import lax
from jax.sharding import PartitionSpec as P

GRID = 256
INNER = 4


time_step = 0.1
coulomb = 30.0
bond_stiffness = 0.2
soften = 1.0
cutoff_sq = 144.0
ewald_beta = 0.32
highest = lax.Precision.HIGHEST


def with_halo(block, sides, width):
    for axis, dim in sides:
        count = lax.axis_size(axis)
        forward = [(i, i + 1) for i in range(count - 1)]
        forward.append((count - 1, 0))
        backward = [(target, source) for source, target in forward]
        low = lax.ppermute(
            lax.slice_in_dim(block, block.shape[dim] - width, None, axis=dim), axis, forward
        )
        high = lax.ppermute(lax.slice_in_dim(block, 0, width, axis=dim), axis, backward)
        block = jnp.concatenate([low, block, high], axis=dim)
    return block


def passed_along(value, axis, steps):
    count = lax.axis_size(axis)
    pairs = [(source, (source + steps) % count) for source in range(count)]
    return lax.ppermute(value, axis, pairs)


def spline_pieces(frac):
    rest = 1.0 - frac
    cube = frac * frac * frac
    square = frac * frac
    return (
        rest * rest * rest / 6.0,
        (3.0 * cube - 6.0 * square + 4.0) / 6.0,
        (-3.0 * cube + 3.0 * square + 3.0 * frac + 1.0) / 6.0,
        cube / 6.0,
    )


def axis_weights(cells, offset, frac, wrapped):
    place = cells[:, None] - offset[None, :]
    if wrapped:
        place = jnp.mod(place, GRID)
    pieces = spline_pieces(frac)
    total = jnp.zeros(place.shape, jnp.float32)
    for order in range(4):
        total = total + jnp.where(place == order, pieces[order][None, :], 0.0)
    return total


def patch_weights(place, offsets, tile_index, pen_index, planes_x, rows_y):
    frac = place - (offsets.astype(jnp.float32) + 1.0)
    cells_x = tile_index * planes_x - 1 + jnp.arange(planes_x + 3, dtype=jnp.int32)
    cells_y = pen_index * rows_y - 1 + jnp.arange(rows_y + 3, dtype=jnp.int32)
    weight_x = axis_weights(cells_x, offsets[0], frac[0], False)
    weight_y = axis_weights(cells_y, offsets[1], frac[1], False)
    depth = axis_weights(jnp.arange(GRID, dtype=jnp.int32), offsets[2], frac[2], True)
    plane = (weight_x[:, None, :] * weight_y[None, :, :]).reshape(-1, place.shape[1])
    return (plane, depth)


def influence(freq_x, freq_y, freq_z):

    def signed(freq):
        return jnp.where(freq > GRID // 2, freq - GRID, freq).astype(jnp.float32)

    def modulus(freq):
        angle = 2.0 * math.pi / GRID * freq.astype(jnp.float32)
        real = (1.0 + 4.0 * jnp.cos(angle) + jnp.cos(2.0 * angle)) / 6.0
        imag = (4.0 * jnp.sin(angle) + jnp.sin(2.0 * angle)) / 6.0
        return 1.0 / (real * real + imag * imag)

    sx, sy, sz = (signed(freq_x), signed(freq_y), signed(freq_z))
    m_sq = (sx[:, None, None] ** 2 + sy[None, :, None] ** 2 + sz[None, None, :] ** 2) / float(
        GRID * GRID
    )
    anchor = (
        (freq_x[:, None, None] == 0) & (freq_y[None, :, None] == 0) & (freq_z[None, None, :] == 0)
    )
    safe = jnp.where(anchor, 1.0, m_sq)
    value = jnp.exp(-((math.pi / ewald_beta) ** 2) * safe) / (math.pi * float(GRID) ** 3 * safe)
    value = (
        value
        * modulus(freq_x)[:, None, None]
        * modulus(freq_y)[None, :, None]
        * modulus(freq_z)[None, None, :]
    )
    return jnp.where(anchor, 0.0, value)


def cas_table(count):
    index = jnp.arange(count, dtype=jnp.int32)
    product = jnp.mod(index[:, None] * index[None, :], count)
    angle = 2.0 * math.pi / count * product.astype(jnp.float32)
    return jnp.cos(angle) + jnp.sin(angle)


def pair_force(table, own, charge, neighbours, bonded, rest):
    near = table[:, neighbours]
    delta = own[:, None, :] - near[:3]
    dist_sq = jnp.sum(delta * delta, axis=0)
    taper = jnp.where(dist_sq < cutoff_sq, (1.0 - dist_sq / cutoff_sq) ** 2, 0.0)
    strength = coulomb * charge[None, :] * near[3] * taper * (dist_sq + soften) ** (-1.5)
    force = jnp.sum(strength[None] * delta, axis=1)
    bond_delta = own[:, None, :] - table[:3][:, bonded]
    length = jnp.sqrt(jnp.sum(bond_delta * bond_delta, axis=0) + soften)
    pull = -bond_stiffness * (length - rest) / length
    return force + jnp.sum(pull[None] * bond_delta, axis=1)


def on_device(
    positions,
    velocities,
    charges,
    inverse_mass,
    export_rows,
    partners,
    bond_partners,
    bond_rest,
    block_offsets,
):
    tile_count = lax.axis_size("tile")
    pen_count = lax.axis_size("pen")
    half_count = lax.axis_size("sub")
    tile_index = lax.axis_index("tile")
    pen_index = lax.axis_index("pen")
    half_index = lax.axis_index("sub")
    atoms = positions.shape[3]
    half_atoms = atoms // half_count
    planes_x = GRID // tile_count
    rows_y = GRID // pen_count
    coords = positions[:, 0, 0]
    speeds = velocities[:, 0, 0]
    charge = charges[0, 0]
    scale = inverse_mass[0, 0]
    neighbours = partners[0, 0]
    bonded = bond_partners[0, 0]
    rest = bond_rest[0, 0]
    shown = export_rows[0, 0]
    first_atom = half_index * half_atoms
    border = jnp.arange(3, dtype=jnp.int32) - 1
    near_x = tile_index + border
    near_y = pen_index + border
    move_x = jnp.where(near_x < 0, -float(GRID), jnp.where(near_x >= tile_count, float(GRID), 0.0))
    move_y = jnp.where(near_y < 0, -float(GRID), jnp.where(near_y >= pen_count, float(GRID), 0.0))
    blank = jnp.zeros((3, 3), jnp.float32)
    image = jnp.stack(
        [
            jnp.broadcast_to(move_x[:, None], (3, 3)),
            jnp.broadcast_to(move_y[None, :], (3, 3)),
            blank,
            blank,
        ]
    )[..., None]
    own_charge = charge[None]
    for step in range(INNER):
        sent = jnp.concatenate(
            [jnp.take(coords, shown, axis=1), jnp.take(charge, shown)[None]], axis=0
        )
        beside_all = with_halo(sent[:, None, None, :], (("tile", 1), ("pen", 2)), 1)
        beside_all = (beside_all + image).reshape(4, -1)
        own_rows = jnp.concatenate([coords, own_charge], axis=0)
        partial_value = pair_force(
            jnp.concatenate([own_rows, beside_all], axis=1),
            coords,
            charge,
            neighbours,
            bonded,
            rest,
        )
        total = lax.psum(partial_value, "sub")
        speeds = speeds + time_step * scale * total
        coords = coords + time_step * speeds
    mine = lax.dynamic_slice_in_dim(coords, first_atom, half_atoms, 1)
    offsets = lax.dynamic_slice_in_dim(block_offsets[:, 0, 0], first_atom, half_atoms, 1)
    half_charge = lax.dynamic_slice_in_dim(charge, first_atom, half_atoms, 0)
    plane, depth = patch_weights(mine, offsets, tile_index, pen_index, planes_x, rows_y)
    local = jnp.einsum("pa,za->pz", plane * half_charge[None, :], depth, precision=highest)
    block = local.reshape(planes_x + 3, rows_y + 3, GRID)
    from_above = passed_along(block[0:1], "tile", -1)
    from_below = passed_along(block[planes_x + 1 :], "tile", 1)
    inner_x = block[1 : planes_x + 1].at[0:2].add(from_below).at[planes_x - 1 :].add(from_above)
    from_right = passed_along(inner_x[:, 0:1], "pen", -1)
    from_left = passed_along(inner_x[:, rows_y + 1 :], "pen", 1)
    core = inner_x[:, 1 : rows_y + 1].at[:, 0:2].add(from_left).at[:, rows_y - 1 :].add(from_right)
    pencil = lax.psum_scatter(core, "sub", scatter_dimension=1, tiled=True)
    table = cas_table(GRID)
    depth_done = jnp.dot(pencil.reshape(-1, GRID), table, precision=highest).reshape(pencil.shape)
    lines = jnp.einsum(
        "ky,xyz->xkz",
        table,
        lax.all_to_all(depth_done, ("pen", "sub"), split_axis=2, concat_axis=1, tiled=True),
        precision=highest,
    )
    slab = lines.shape[2]
    depth_rows = lax.axis_index(("pen", "sub")) * slab + jnp.arange(slab, dtype=jnp.int32)
    every_row = jnp.arange(GRID, dtype=jnp.int32)
    wide = lax.all_to_all(lines, "tile", split_axis=1, concat_axis=0, tiled=True)
    spectrum = jnp.einsum("kx,xyz->kyz", table, wide, precision=highest)
    share_y = wide.shape[1]
    column_rows = tile_index * share_y + jnp.arange(share_y, dtype=jnp.int32)
    weighted = spectrum * influence(every_row, column_rows, depth_rows)
    turned = jnp.einsum("kx,xyz->kyz", table, weighted, precision=highest)
    back = lax.all_to_all(turned, "tile", split_axis=0, concat_axis=1, tiled=True)
    rows_back = jnp.einsum("ky,xyz->xkz", table, back, precision=highest)
    returned = lax.all_to_all(rows_back, ("pen", "sub"), split_axis=1, concat_axis=2, tiled=True)
    potential_grid = jnp.dot(returned.reshape(-1, GRID), table, precision=highest).reshape(
        returned.shape
    )
    full_rows = lax.all_gather(potential_grid, "sub", axis=1, tiled=True)
    framed = with_halo(full_rows, (("tile", 0), ("pen", 1)), 2)[1:, 1:]
    values = jnp.dot(framed.reshape(-1, GRID), depth, precision=highest)
    potential = jnp.sum(values * plane, axis=0)
    return (coords[:, None, None, :], speeds[:, None, None, :], potential[None, None, :])


def solution(mesh):
    placed = (
        P("rep", "tile", "pen", None),
        P("rep", "tile", "pen", None),
        P(("rep", "tile"), "pen", None),
        P(("rep", "tile"), "pen", None),
        P(("rep", "tile"), "pen", None),
        P(("rep", "tile"), "pen", "sub", None),
        P(("rep", "tile"), "pen", "sub", None),
        P(("rep", "tile"), "pen", "sub", None),
        P("rep", "tile", "pen", None),
    )
    return jax.shard_map(
        on_device,
        mesh=mesh,
        in_specs=placed,
        out_specs=(
            P("rep", "tile", "pen", None),
            P("rep", "tile", "pen", None),
            P(("rep", "tile"), "pen", "sub"),
        ),
        check_vma=False,
    )
```

profile of v0, /device:TPU:1, one launch (start us, length us, event | category | flops | bytes accessed | tf_op | source)
XLA Modules:
  0.0 1107.9 jit_solution(3997656631664268906)
XLA Ops:
  30.3 54.4 %gather_fusion = f32[16384,4]{1,0:T(8,128)} fusion(f32[4,1664]{0,1:T(8,128)S(1)} %copy.139, s32[16384]{0:T(1024)S(1)} %broadcast_clamp_fusion), kind=kCustom, calls=%fused_computation.5 | custom fusion | bytes 589824 | tf_op jit(solution)/shard_map/gather | solution.py:112
  108.2 54.4 %gather_fusion.2 = f32[16384,4]{1,0:T(8,128)} fusion(f32[4,1664]{0,1:T(8,128)S(1)} %copy.146, s32[16384]{0:T(1024)S(1)} %broadcast_clamp_fusion), kind=kCustom, calls=%fused_computation.7 | custom fusion | bytes 589824 | tf_op jit(solution)/shard_map/gather | solution.py:112
  186.6 54.4 %gather_fusion.4 = f32[16384,4]{1,0:T(8,128)} fusion(f32[4,1664]{0,1:T(8,128)S(1)} %copy.153, s32[16384]{0:T(1024)S(1)} %broadcast_clamp_fusion), kind=kCustom, calls=%fused_computation.9 | custom fusion | bytes 589824 | tf_op jit(solution)/shard_map/gather | solution.py:112
  263.7 54.4 %gather_fusion.6 = f32[16384,4]{1,0:T(8,128)} fusion(f32[4,1664]{0,1:T(8,128)S(1)} %copy.160, s32[16384]{0:T(1024)S(1)} %broadcast_clamp_fusion), kind=kCustom, calls=%fused_computation.11 | custom fusion | bytes 589824 | tf_op jit(solution)/shard_map/gather | solution.py:112
  323.6 16.6 %psum.31 = f32[3,512]{1,0:T(4,128)S(1)} all-reduce(f32[3,512]{1,0:T(4,128)S(1)} %add.620), channel_id=1, replica_groups=mesh['rep'=2,'tile'=4,'pen'=2,'sub'=2] {'sub'}, use_global_device_ids=true, to_apply=%region_19.22 | all-reduce | flops 1536 | bytes 12288 | tf_op jit(solution)/shard_map/psum | solution.py:184
  345.8 10.2 mul.739
  356.0 10.3 fusion
  369.9 5.9 slice.278
  380.0 9.4 slice.217
  407.2 15.9 %reduce-scatter.2.cloned.1.call-done = f32[64,64,256]{2,1,0:T(8,128)} async-done(((f32[64,128,256]{2,1,0:T(8,128)}), f32[64,64,256]{2,1,0:T(8,128)}) %reduce-scatter.2.cloned.1.call-update) | async-done | bytes 4194320 | tf_op jit(solution)/shard_map/reduce_scatter | solution.py:199
  423.1 8.7 fusion.13
  431.8 9.1 copy.166
  441.0 8.6 reshape.1011
  449.6 53.0 %all_to_all.69 = f32[4,1,262144]{2,1,0:T(1,128)} all-to-all(f32[4,1,262144]{2,1,0:T(1,128)} %reshape.1011), channel_id=1, replica_groups=mesh['rep'=2,'tile'=4,'pen'=2,'sub'=2] {'pen','sub'}, dimensions={0} | all-to-all | bytes 8388608 | tf_op jit(solution)/shard_map/all_to_all | solution.py:205
  503.1 16.7 %reduce.8 = f32[4,262144]{1,0:T(4,128)} reduce(f32[4,1,262144]{2,1,0:T(1,128)} %all_to_all.69, f32[]{:T(128)} %broadcast.1188), dimensions={1}, to_apply=%all_to_all.50.reduce_sub_computation | reduce | bytes 8388612 | tf_op jit(solution)/shard_map/all_to_all | solution.py:205
  519.7 9.3 reshape.1012
  529.0 12.1 %copy.197 = f32[64,64,4,64]{1,2,3,0:T(4,128)} copy(f32[64,64,4,64]{1,0,3,2:T(8,128)} %bitcast.202) | data formatting | bytes 8388608 | tf_op jit(solution)/shard_map/all_to_all | solution.py:205
  541.1 8.7 all_to_all.53
  549.8 8.7 convolution_bitcast_fusion.1
  558.5 9.1 copy.168
  567.7 8.6 reshape.1013
  581.6 92.4 %all-to-all-done.1 = f32[4,1,262144]{2,1,0:T(1,128)} async-done(((f32[4,1,262144]{2,1,0:T(1,128)}), f32[4,1,262144]{2,1,0:T(1,128)}, u32[]{:S(2)}, u32[]{:S(2)}) %all-to-all-start.1) | async-done | bytes 4194336 | tf_op jit(solution)/shard_map/all_to_all | solution.py:211
  674.0 16.2 %reduce.9 = f32[4,262144]{1,0:T(4,128)} reduce(f32[4,1,262144]{2,1,0:T(1,128)} %all-to-all-done.1, f32[]{:T(128)} %broadcast.1188), dimensions={1}, to_apply=%all_to_all.54.reduce_sub_computation | reduce | bytes 8388612 | tf_op jit(solution)/shard_map/all_to_all | solution.py:211
  690.3 9.3 reshape.1014
  699.6 10.0 copy.169
  709.5 9.0 reshape.1006
  718.5 7.0 fusion.23
  728.1 6.5 fusion.24
  734.6 9.3 copy.170
  743.9 8.6 reshape.1015
  752.6 97.8 %all_to_all.70 = f32[4,1,262144]{2,1,0:T(1,128)} all-to-all(f32[4,1,262144]{2,1,0:T(1,128)} %reshape.1015), channel_id=1, replica_groups=mesh['rep'=2,'tile'=4,'pen'=2,'sub'=2] {'tile'}, dimensions={0} | all-to-all | bytes 8388608 | tf_op jit(solution)/shard_map/all_to_all | solution.py:217
  850.4 16.2 %reduce.10 = f32[4,262144]{1,0:T(4,128)} reduce(f32[4,1,262144]{2,1,0:T(1,128)} %all_to_all.70, f32[]{:T(128)} %broadcast.1188), dimensions={1}, to_apply=%all_to_all.58.reduce_sub_computation | reduce | bytes 8388612 | tf_op jit(solution)/shard_map/all_to_all | solution.py:217
  866.6 9.3 reshape.1016
  875.9 10.0 copy.171
  885.9 8.8 all_to_all.61
  894.6 8.7 convolution_bitcast_fusion
  903.3 9.1 copy.172
  912.5 8.6 reshape.1017
  921.1 54.7 %all_to_all.71 = f32[4,1,262144]{2,1,0:T(1,128)} all-to-all(f32[4,1,262144]{2,1,0:T(1,128)} %reshape.1017), channel_id=1, replica_groups=mesh['rep'=2,'tile'=4,'pen'=2,'sub'=2] {'pen','sub'}, dimensions={0} | all-to-all | bytes 8388608 | tf_op jit(solution)/shard_map/all_to_all | solution.py:219
  975.8 16.7 %reduce.11 = f32[4,262144]{1,0:T(4,128)} reduce(f32[4,1,262144]{2,1,0:T(1,128)} %all_to_all.71, f32[]{:T(128)} %broadcast.1188), dimensions={1}, to_apply=%all_to_all.62.reduce_sub_computation | reduce | bytes 8388612 | tf_op jit(solution)/shard_map/all_to_all | solution.py:219
  992.5 9.3 reshape.1018
  1001.7 12.1 %copy.196 = f32[64,4,64,64]{3,1,2,0:T(4,128)} copy(f32[64,4,64,64]{3,0,2,1:T(8,128)} %bitcast.208) | data formatting | bytes 8388608 | tf_op jit(solution)/shard_map/all_to_all | solution.py:219
  1013.8 8.7 dot_general.32
  1022.6 8.7 fusion.9
  1031.3 19.1 %all-gather.2.cloned.1.call-done = f32[64,128,256]{2,1,0:T(8,128)} async-done(((f32[64,64,256]{2,1,0:T(8,128)}), f32[64,128,256]{2,1,0:T(8,128)}) %all-gather.2.cloned.1.call-update) | async-done | bytes 8388624 | tf_op jit(solution)/shard_map/all_gather | solution.py:223
  1055.0 6.2 collective-permute-done.20
  1078.7 10.2 reshape.877
  1088.9 12.0 %fusion.4 = f32[256]{0:T(256)} fusion(f32[8777,256]{1,0:T(8,128)} %mul.739, f32[8777,256]{1,0:T(8,128)} %reshape.877, f32[256]{0:T(256)S(1)} %bitcast.265, f32[256]{0:T(256)S(1)} %bitcast.267, f32[256]{0:T(256)S(1)} %bitcast.263, f32[256]{0:T(256)S(1)} %bitcast.261, s32[256]{0:T(256)S(1)} %bitcast.258), kind=kOutput, calls=%fused_computation.25 | convolution fusion | flops 6908514304 | bytes 17981440 | tf_op jit(solution)/shard_map/dot_general | solution.py:225
  (222 shorter events, 159.5 us)
Async XLA Ops:
  7.2 95.6 %copy-start = (s32[3,1,1,512]{3,2,1,0:T(1,128)S(1)}, s32[3,1,1,512]{3,2,1,0:T(1,128)}, u32[]{:S(2)}) copy-start(s32[3,1,1,512]{3,2,1,0:T(1,128)} %param.29) | copy-start | bytes 18436
  7.2 415.9 %reduce-scatter.2.cloned.1.call-start = ((), (), s32[]{:S(2)}) async-start(), calls=%async_computation.5 | async-start | bytes 12582912 | tf_op jit(solution)/shard_map/reduce_scatter | solution.py:199
  11.8 84.1 %copy-start.9 = (f32[3,1,1,512]{3,2,1,0:T(1,128)S(1)}, f32[3,1,1,512]{3,2,1,0:T(1,128)}, u32[]{:S(2)}) copy-start(f32[3,1,1,512]{3,2,1,0:T(1,128)} %param.21) | copy-start | bytes 18436
  11.8 84.1 %copy-start.10 = (f32[3,1,1,512]{3,2,1,0:T(1,128)S(1)}, f32[3,1,1,512]{3,2,1,0:T(1,128)}, u32[]{:S(2)}) copy-start(f32[3,1,1,512]{3,2,1,0:T(1,128)} %param.22) | copy-start | bytes 18436
  12.6 6.1 collective-permute-start.1
  16.8 4.2 collective-permute-start
  17.7 86.4 %copy-start.2 = (f32[1,1,512]{2,1,0:T(1,128)S(1)}, f32[1,1,512]{2,1,0:T(1,128)}, u32[]{:S(2)}) copy-start(f32[1,1,512]{2,1,0:T(1,128)} %param.23) | copy-start | bytes 6148
  21.0 2.5 collective-permute-start.3
  22.2 2.5 collective-permute-start.2
  29.2 78.6 %copy-start.5 = (f32[1,1,2,512]{3,2,1,0:T(2,128)S(1)}, f32[1,1,2,512]{3,2,1,0:T(2,128)}, u32[]{:S(2)}) copy-start(f32[1,1,2,512]{3,2,1,0:T(2,128)} %param.28) | copy-start | bytes 12292
  96.8 2.5 collective-permute-start.5
  97.0 4.2 collective-permute-start.4
  101.3 2.5 collective-permute-start.7
  101.5 2.5 collective-permute-start.6
  174.4 2.5 collective-permute-start.9
  174.4 4.3 collective-permute-start.8
  178.7 2.5 collective-permute-start.11
  179.9 2.5 collective-permute-start.10
  252.5 2.5 collective-permute-start.13
  252.5 4.3 collective-permute-start.12
  256.8 2.5 collective-permute-start.15
  257.1 2.5 collective-permute-start.14
  340.8 0.6 copy-start.6
  366.3 3.5 copy-start.3
  369.8 19.6 %collective-permute-start.16 = (f32[2,131,256]{2,1,0:T(8,128)S(1)}, f32[2,131,256]{2,1,0:T(8,128)S(1)}, u32[]{:S(2)}, u32[]{:S(2)}) collective-permute-start(f32[2,131,256]{2,1,0:T(8,128)S(1)} %slice.220), channel_id=1, source_target_pairs={{0,4},{4,8},{8,12},{12,0},{1,5},{5,9},{9,13},{13,1},{2,6},{6,10},{... | collective-permute-start | bytes 804872 | tf_op jit(solution)/shard_map/ppermute | solution.py:38
  376.7 13.5 %collective-permute-start.17 = (f32[1,131,256]{2,1,0:T(8,128)S(1)}, f32[1,131,256]{2,1,0:T(8,128)S(1)}, u32[]{:S(2)}, u32[]{:S(2)}) collective-permute-start(f32[1,131,256]{2,1,0:T(8,128)S(1)} %slice_bitcast_fusion), channel_id=1, source_target_pairs={{0,12},{4,0},{8,4},{12,8},{1,13},{5,1},{9,5},{13,9},{2,14},{6,2},{... | collective-permute-start | bytes 402440 | tf_op jit(solution)/shard_map/ppermute | solution.py:38
  392.9 7.4 collective-permute-start.18
  399.9 3.2 collective-permute-start.19
  401.4 3.2 copy-start.4
  576.3 97.7 %all-to-all-start.1 = ((f32[4,1,262144]{2,1,0:T(1,128)}), f32[4,1,262144]{2,1,0:T(1,128)}, u32[]{:S(2)}, u32[]{:S(2)}) async-start(f32[4,1,262144]{2,1,0:T(1,128)} %reshape.1013), calls=%async_computation.2 | async-start | bytes 8388608 | tf_op jit(solution)/shard_map/all_to_all | solution.py:211
  581.2 469.3 %all-gather.2.cloned.1.call-start = ((), (), s32[]{:S(2)}) async-start(), calls=%async_computation.6 | async-start | bytes 12582912 | tf_op jit(solution)/shard_map/all_gather | solution.py:223
  1051.5 9.7 collective-permute-start.20
  1053.1 13.5 %collective-permute-start.21 = (f32[2,128,256]{2,1,0:T(8,128)S(1)}, f32[2,128,256]{2,1,0:T(8,128)S(1)}, u32[]{:S(2)}, u32[]{:S(2)}) collective-permute-start(f32[2,128,256]{2,1,0:T(8,128)S(1)} %get-tuple-element.78), channel_id=1, source_target_pairs={{4,0},{8,4},{12,8},{0,12},{5,1},{9,5},{13,9},{1,13},{6,2},{10,6},{... | collective-permute-start | bytes 786440 | tf_op jit(solution)/shard_map/ppermute | solution.py:30
  1061.2 7.0 copy-start.8
  1061.2 7.6 copy-start.7
  1066.7 4.0 collective-permute-start.22
  1067.7 5.9 collective-permute-start.23
  1078.7 22.2 %copy-start.1 = (s32[3,1,1,512]{3,2,1,0:T(1,128)S(1)}, s32[3,1,1,512]{3,2,1,0:T(1,128)}, u32[]{:S(2)}) copy-start(s32[3,1,1,512]{3,2,1,0:T(1,128)} %param.29) | copy-start | bytes 18436
Sparse Core Ops, SparseCore 0:
  407.3 15.7 reduce-scatter.1
  1031.4 18.9 all-gather.1
where the time goes:
time: 1120 us; the launch traced here: 1110 us
  local copies, waits for them, and re-layouts  506 us (45%)
  blocking collectives  238 us (21%)
  waiting for transfers between devices  157 us (14%)
  other arithmetic  91.3 us (8%)
  matrix products  70.6 us (6%)
  starting transfers between devices  29.5 us (3%)
  between operations  15 us (1%)
    gather x8, local copies, waits for them, and re-layouts, pair_force(): near = table[:, neighbours]  239 us
    all_to_all x1, blocking collectives, on_device(): lax.all_to_all(turned, 'tile', split_axis=0, concat_axis=1, tiled=True)  97.8 us
    unnamed x41, local copies, waits for them, and re-layouts  92.9 us
    all_to_all x1, waiting for transfers between devices, on_device(): lax.all_to_all(lines, 'tile', split_axis=1, concat_axis=0, tiled=True)  92.4 us
    all_to_all x1, blocking collectives, on_device(): lax.all_to_all(rows_back, ('pen', 'sub'), split_axis=1, concat_axis=2, ti...  54.7 us
    all_to_all x1, blocking collectives, on_device(): lax.all_to_all(depth_done, ('pen', 'sub'), split_axis=2, concat_axis=1, t...  53 us
    psum x4, blocking collectives, on_device(): total = lax.psum(partial_value, 'sub')  32.8 us
  transfers between devices with their start and end apart: 27, of which 23 were waited for; matrix products, arithmetic and copies ran while one was open for 3% of the time, Pallas kernels for 0%

commit v1 on v0

v1 whole, which is shorter than its diff:
```python
import functools
import math

import jax
import jax.numpy as jnp
import numpy as np
from jax import lax
from jax.experimental import pallas as pl
from jax.experimental.pallas import tpu as pltpu
from jax.sharding import PartitionSpec as P

GRID = 256
INNER = 4
LANES = 128

time_step = 0.1
coulomb = 30.0
bond_stiffness = 0.2
soften = 1.0
cutoff_sq = 144.0
ewald_beta = 0.32

f32 = jnp.float32
bf16 = jnp.bfloat16


def lane_gather(rows, low):
    return jnp.take_along_axis(rows, low, axis=1, mode="promise_in_bounds")


def shown_rows(state, shown):
    index = jnp.broadcast_to(shown, (8, shown.shape[1]))
    low, high = index & (LANES - 1), index >> 7
    total = jnp.zeros((8, shown.shape[1]), f32)
    for block in range(state.shape[1] // LANES):
        part = lane_gather(state[:, block * LANES : (block + 1) * LANES], low)
        total = jnp.where(high == block, part, total)
    return total[:4]


def export_kernel(state_ref, shown_ref, sent_ref):
    sent_ref[...] = shown_rows(state_ref[...], shown_ref[...])


def step_kernel(
    place_ref, state_ref, beside_ref, shown_ref, partners_ref, bonds_ref, rest_ref,
    out_ref, sent_ref, table, *, tile_count, pen_count,
):
    atoms = state_ref.shape[1]
    own_blocks = atoms // LANES
    halo_blocks = beside_ref.shape[2] // LANES
    tile_index, pen_index = place_ref[0], place_ref[1]
    blocks = list(range(own_blocks))
    for block in range(own_blocks):
        for row in range(4):
            table[block * 4 + row] = jnp.broadcast_to(
                state_ref[row : row + 1, block * LANES : (block + 1) * LANES], (8, LANES)
            )
    for i in range(3):
        near_x = tile_index + (i - 1)
        move_x = jnp.where(near_x < 0, -float(GRID), jnp.where(near_x >= tile_count, float(GRID), 0.0))
        for j in range(3):
            if i == 1 and j == 1:
                continue
            near_y = pen_index + (j - 1)
            move_y = jnp.where(near_y < 0, -float(GRID), jnp.where(near_y >= pen_count, float(GRID), 0.0))
            patch = beside_ref[j * 3 + i]
            for part in range(halo_blocks):
                block = own_blocks + (i * 3 + j) * halo_blocks + part
                blocks.append(block)
                for row in range(4):
                    line = patch[row : row + 1, part * LANES : (part + 1) * LANES]
                    if row == 0:
                        line = line + move_x
                    if row == 1:
                        line = line + move_y
                    table[block * 4 + row] = jnp.broadcast_to(line, (8, LANES))

    def fetch(index, rows, among):
        low, high = index & (LANES - 1), index >> 7
        found = [jnp.zeros((8, LANES), f32) for _ in range(rows)]
        for block in among:
            hit = high == block
            for row in range(rows):
                found[row] = jnp.where(hit, lane_gather(table[block * 4 + row], low), found[row])
        return found

    for c in range(own_blocks):
        lanes = slice(c * LANES, (c + 1) * LANES)
        own = [jnp.broadcast_to(state_ref[r : r + 1, lanes], (8, LANES)) for r in range(4)]

        def slots(g, force, lanes=lanes, own=own):
            index = partners_ref[pl.ds(pl.multiple_of(g * 8, 8), 8), lanes]
            near = fetch(index, 4, blocks)
            delta = [own[r] - near[r] for r in range(3)]
            dist_sq = delta[0] * delta[0] + delta[1] * delta[1] + delta[2] * delta[2]
            taper = 1.0 - dist_sq / cutoff_sq
            taper = jnp.where(dist_sq < cutoff_sq, taper * taper, 0.0)
            root = lax.rsqrt(dist_sq + soften)
            strength = coulomb * own[3] * near[3] * taper * (root * root * root)
            return tuple(force[r] + strength * delta[r] for r in range(3))

        def bonded(g, force, lanes=lanes, own=own):
            rows = pl.ds(pl.multiple_of(g * 8, 8), 8)
            near = fetch(bonds_ref[rows, lanes], 3, range(own_blocks))
            delta = [own[r] - near[r] for r in range(3)]
            root = lax.rsqrt(delta[0] * delta[0] + delta[1] * delta[1] + delta[2] * delta[2] + soften)
            pull = -bond_stiffness * (1.0 - rest_ref[rows, lanes] * root)
            return tuple(force[r] + pull * delta[r] for r in range(3))

        force = tuple(jnp.zeros((8, LANES), f32) for _ in range(3))
        force = lax.fori_loop(0, partners_ref.shape[0] // 8, slots, force)
        force = lax.fori_loop(0, bonds_ref.shape[0] // 8, bonded, force)
        scale = state_ref[7:8, lanes]
        for r in range(3):
            total = jnp.sum(force[r], axis=0, keepdims=True)
            speed = state_ref[4 + r : 5 + r, lanes] + time_step * scale * total
            out_ref[4 + r : 5 + r, lanes] = speed
            out_ref[r : r + 1, lanes] = state_ref[r : r + 1, lanes] + time_step * speed
        out_ref[3:4, lanes] = state_ref[3:4, lanes]
        out_ref[7:8, lanes] = scale
    sent_ref[...] = shown_rows(out_ref[...], shown_ref[...])


def split(value):
    high = value.astype(bf16)
    return high, (value - high.astype(f32)).astype(bf16)


def product(left, right, turned=False):
    dims = (((1,), (1 if turned else 0,)), ((), ()))

    def dot(a, b):
        return lax.dot_general(a, b, dims, preferred_element_type=f32)

    return dot(left[0], right[0]) + (dot(left[0], right[1]) + dot(left[1], right[0]))


def spline(place, frac):
    rest = 1.0 - frac
    square = frac * frac
    cube = square * frac
    pieces = (
        rest * rest * rest / 6.0,
        (3.0 * cube - 6.0 * square + 4.0) / 6.0,
        (-3.0 * cube + 3.0 * square + 3.0 * frac + 1.0) / 6.0,
        cube / 6.0,
    )
    total = jnp.zeros(place.shape, f32)
    for order in range(4):
        total = jnp.where(place == order, pieces[order], total)
    return total


def mesh_kernel(
    first_ref, lines_ref, squares_ref, atoms_ref, mine_ref, cas_ref, wide_ref, tall_ref, along_ref, across_ref,
    out_ref, grid, wx, wy, wz, *, planes, chunk, keep,
):
    tiles, share, deep = grid.shape[0], grid.shape[1], grid.shape[2]
    atoms = atoms_ref.shape[2]
    first = first_ref[0]

    def cells(offset, count):
        return lax.broadcasted_iota(jnp.int32, (count, atoms), 0) - offset

    def prepare(s):
        own = atoms_ref[s]
        offset = own[3:6].astype(jnp.int32)
        depth = spline(cells(offset[2:3], GRID) & (GRID - 1), own[2:3])
        return product((cas_ref[0], cas_ref[1]), split(depth))

    def tile_of(s):
        apart = first_ref[1] - s
        return jnp.where(apart < 0, apart + tiles, apart)

    def spread(s, carry):
        t = tile_of(s)
        own = atoms_ref[s]
        offset = own[3:6].astype(jnp.int32)
        wx[t] = spline(cells(offset[0:1] - (t * planes - 1), deep), own[0:1])
        rows = spline(cells(offset[1:2], GRID) & (GRID - 1), own[1:2])
        wy[t] = product((mine_ref[0], mine_ref[1]), split(rows))
        depth = prepare(s)
        if keep:
            high, low = split(depth)
            wz[t, 0] = high
            wz[t, 1] = low
        charged = split(depth * own[6:7])
        for c in range(0, share, chunk):
            pieces = [wx[t] * wy[t, k : k + 1, :] for k in range(c, c + chunk)]
            plane = split(jnp.concatenate(pieces, axis=0))
            grid[t, c : c + chunk] = product(plane, charged, True).reshape(chunk, deep, GRID)
        return carry

    lax.fori_loop(0, tiles, spread, 0)

    def transform(k, carry):
        line = grid[:, k].reshape(tiles * deep, GRID)
        spectrum = product((wide_ref[0], wide_ref[1]), split(line))
        m_sq = along_ref[...] + squares_ref[first + k]
        anchor = m_sq == 0.0
        value = across_ref[...] * lines_ref[first + k] / jnp.where(anchor, 1.0, m_sq)
        weighted = spectrum * jnp.where(anchor, 0.0, value)
        back = product((tall_ref[0], tall_ref[1]), split(weighted))
        grid[:, k] = back.reshape(tiles, deep, GRID)
        return carry

    lax.fori_loop(0, share, transform, 0)

    def read(s, carry):
        t = tile_of(s)
        if keep:
            depth = (wz[t, 0], wz[t, 1])
        else:
            depth = split(prepare(s))
        total = jnp.zeros((deep, atoms), f32)
        for c in range(0, share, chunk):
            line = split(grid[t, c : c + chunk].reshape(chunk * deep, GRID))
            values = product(line, depth)
            for k in range(chunk):
                total = total + values[k * deep : (k + 1) * deep] * wy[t, c + k : c + k + 1, :]
        out_ref[s] = jnp.sum(total * wx[t], axis=0, keepdims=True)
        return carry

    lax.fori_loop(0, tiles, read, 0)


def halves(table):
    table = jnp.asarray(table.astype(np.float32))
    return jnp.stack(split(table))


def tables(tiles, planes, deep):
    index = np.arange(GRID)
    angle = 2.0 * math.pi / GRID * np.mod(index[:, None] * index[None, :], GRID)
    cas = np.cos(angle) + np.sin(angle)
    place = np.mod(np.arange(tiles)[:, None] * planes - 1 + np.arange(deep)[None, :], GRID).reshape(-1)
    wide = cas[:, place]
    signed = np.where(index > GRID // 2, index - GRID, index).astype(np.float64)
    turn = 2.0 * math.pi / GRID * index
    real = (1.0 + 4.0 * np.cos(turn) + np.cos(2.0 * turn)) / 6.0
    imag = (4.0 * np.sin(turn) + np.sin(2.0 * turn)) / 6.0
    square = signed**2 / float(GRID * GRID)
    line = np.exp(-((math.pi / ewald_beta) ** 2) * square) / (real * real + imag * imag)
    along = square[:, None] + square[None, :]
    across = line[:, None] * line[None, :] / (math.pi * float(GRID) ** 3)
    return cas, wide, line.astype(np.float32), square.astype(np.float32), along.astype(np.float32), across.astype(np.float32)


def passed_along(value, axis, steps):
    count = lax.axis_size(axis)
    pairs = [(source, (source + steps) % count) for source in range(count)]
    return lax.ppermute(value, axis, pairs)


def on_device(
    positions, velocities, charges, inverse_mass, export_rows, partners, bond_partners, bond_rest, block_offsets,
):
    tile_count = lax.axis_size("tile")
    pen_count = lax.axis_size("pen")
    half_count = lax.axis_size("sub")
    patches = tile_count * pen_count
    tile_index = lax.axis_index("tile")
    pen_index = lax.axis_index("pen")
    atoms = positions.shape[3]
    exported = export_rows.shape[2]
    planes = GRID // tile_count
    place = jnp.stack([tile_index, pen_index]).astype(jnp.int32)
    state = jnp.concatenate(
        [positions[:, 0, 0], charges[0], velocities[:, 0, 0], inverse_mass[0]], axis=0
    )
    shown = export_rows[0]
    neighbours = lax.all_gather(
        jnp.concatenate([partners[0, 0], bond_partners[0, 0]], axis=0), "sub", axis=0
    )
    rest = lax.all_gather(bond_rest[0, 0], "sub", axis=0, tiled=True)
    slots = partners.shape[2]
    near = neighbours[:, :slots].reshape(-1, atoms)
    bonds = neighbours[:, slots:].reshape(-1, atoms)
    fill = -bonds.shape[0] % 8
    self_rows = jnp.broadcast_to(jnp.arange(atoms, dtype=jnp.int32), (fill, atoms))
    bonds = jnp.concatenate([bonds, self_rows], axis=0)
    rest = jnp.concatenate([rest, jnp.ones((fill, atoms), f32)], axis=0)
    vmem = pl.BlockSpec(memory_space=pltpu.VMEM)
    smem = pl.BlockSpec(memory_space=pltpu.SMEM)
    sent_shape = jax.ShapeDtypeStruct((4, exported), f32)
    sent = pl.pallas_call(
        export_kernel, out_shape=sent_shape, in_specs=[vmem, vmem], out_specs=vmem
    )(state, shown)
    columns = (atoms + 9 * exported) // LANES
    step_call = pl.pallas_call(
        functools.partial(step_kernel, tile_count=tile_count, pen_count=pen_count),
        out_shape=(jax.ShapeDtypeStruct(state.shape, f32), sent_shape),
        in_specs=[smem] + [vmem] * 6,
        out_specs=(vmem, vmem),
        scratch_shapes=[pltpu.VMEM((columns * 4, 8, LANES), f32)],
    )
    for step in range(INNER):
        column = jnp.stack([passed_along(sent, "tile", 1), sent, passed_along(sent, "tile", -1)])
        low = passed_along(column, "pen", 1)
        high = low if pen_count == 2 else passed_along(column, "pen", -1)
        beside = jnp.concatenate([low, column, high], axis=0)
        state, sent = step_call(place, state, beside, shown, near, bonds, rest)
    coords, speeds = state[0:3], state[4:7]
    offsets = block_offsets[:, 0, 0].astype(f32)
    packed = jnp.concatenate([coords - (offsets + 1.0), offsets, state[3:4], state[3:4]], axis=0)
    row = jnp.concatenate(
        [packed] + [passed_along(packed, "pen", step) for step in range(1, pen_count)], axis=1
    )
    every = jnp.stack([row] + [passed_along(row, "tile", step) for step in range(1, tile_count)])
    share = GRID // (patches * half_count)
    chunk = math.gcd(share, 8)
    unit = 8 if chunk % 2 == 0 else 16
    deep = -(-(planes + 3) // unit) * unit
    wide_atoms = pen_count * atoms
    keep = patches * atoms * GRID * 4 <= 8 * 1024 * 1024
    cas, wide, line, square, along, across = tables(tile_count, planes, deep)
    start = (lax.axis_index(("tile", "pen", "sub")) * share).astype(jnp.int32)
    first = jnp.stack([start, tile_index.astype(jnp.int32)])
    partial_value = pl.pallas_call(
        functools.partial(mesh_kernel, planes=planes, chunk=chunk, keep=keep),
        out_shape=jax.ShapeDtypeStruct((tile_count, 1, wide_atoms), f32),
        in_specs=[smem] * 3 + [vmem] * 7,
        out_specs=vmem,
        scratch_shapes=[
            pltpu.VMEM((tile_count, share, deep, GRID), f32),
            pltpu.VMEM((tile_count, deep, wide_atoms), f32),
            pltpu.VMEM((tile_count, share, wide_atoms), f32),
            pltpu.VMEM((tile_count if keep else 1, 2, GRID, wide_atoms), bf16),
        ],
        compiler_params=pltpu.CompilerParams(vmem_limit_bytes=60 * 1024 * 1024),
    )(
        first, jnp.asarray(line), jnp.asarray(square), every,
        lax.dynamic_slice_in_dim(halves(cas), start, share, axis=1), halves(cas), halves(wide), halves(wide.T), jnp.asarray(along), jnp.asarray(across),
    )
    sums = partial_value[0]
    for step in range(1, tile_count):
        sums = sums + passed_along(partial_value[step], "tile", -step)
    own = sums[:, :atoms]
    for step in range(1, pen_count):
        own = own + passed_along(sums[:, step * atoms : (step + 1) * atoms], "pen", -step)
    half = lax.axis_index("sub")
    width = atoms // half_count
    potential = lax.dynamic_slice_in_dim(own, half * width, width, 1)
    for step in range(1, half_count):
        other = (half + step) % half_count
        potential = potential + passed_along(
            lax.dynamic_slice_in_dim(own, other * width, width, 1), "sub", step
        )
    potential = potential.reshape(-1)
    return (coords[:, None, None, :], speeds[:, None, None, :], potential[None, None, :])


def solution(mesh):
    placed = (
        P("rep", "tile", "pen", None),
        P("rep", "tile", "pen", None),
        P(("rep", "tile"), "pen", None),
        P(("rep", "tile"), "pen", None),
        P(("rep", "tile"), "pen", None),
        P(("rep", "tile"), "pen", "sub", None),
        P(("rep", "tile"), "pen", "sub", None),
        P(("rep", "tile"), "pen", "sub", None),
        P("rep", "tile", "pen", None),
    )
    return jax.shard_map(
        on_device,
        mesh=mesh,
        in_specs=placed,
        out_specs=(
            P("rep", "tile", "pen", None),
            P("rep", "tile", "pen", None),
            P(("rep", "tile"), "pen", "sub"),
        ),
        check_vma=False,
    )
```

time: 1120 us -> 143 us (0.13)
  local copies, waits for them, and re-layouts: 506 us -> 11.9 us
  blocking collectives: 238 us -> 4.62 us
  waiting for transfers between devices: 157 us -> 19.5 us
  other arithmetic: 91.3 us -> 5.9 us
  matrix products: 70.6 us -> 0 us
  Pallas kernels: 0 us -> 63.4 us
  between operations: 15 us -> 0.76 us
    gather x17 -> x0, local copies, waits for them, and re-layouts: 254 us -> none  [the longest x8 239 us: pair_force(): near = table[:, neighbours]]
    all_to_all x3 -> x0, blocking collectives: 206 us -> none  [the longest x1 97.8 us: on_device(): lax.all_to_all(turned, 'tile', split_axis=0, concat_axis=1, tiled=True)]
    all_to_all x1 -> x0, waiting for transfers between devices: 92.4 us -> none  [on_device(): lax.all_to_all(lines, 'tile', split_axis=1, concat_axis=0, tiled=True)]
    unnamed x41 -> x45, local copies, waits for them, and re-layouts: 92.9 us -> 7.84 us
    all_to_all x4 -> x0, other arithmetic: 65.8 us -> none  [the longest x1 16.7 us: on_device(): lax.all_to_all(rows_back, ('pen', 'sub'), split_axis=1, concat_axis=2, ti...]
    pallas_call x0 -> x6, Pallas kernels: none -> 63.4 us  [the longest x1 36.7 us: on_device(): pl.pallas_call(functools.partial(mesh_kernel, planes=planes, chunk=chunk,...]
    all_to_all x7 -> x0, local copies, waits for them, and re-layouts: 62.1 us -> none  [the longest x3 21.3 us: on_device(): lax.all_to_all(depth_done, ('pen', 'sub'), split_axis=2, concat_axis=1, t...]
    dot_general x6 -> x0, matrix products: 57 us -> none  [the longest x1 12 us: on_device(): values = jnp.dot(framed.reshape(-1, GRID), depth, precision=highest)]
  transfers between devices with their start and end apart: 27 -> 21, of which waited for: 23 -> 13; matrix products, arithmetic and copies ran while one was open for 3% -> 4% of each run, Pallas kernels for 0% -> 0%
where the time goes in v1:
time: 143 us; the launch traced here: 142 us
  Pallas kernels  63.4 us (44%)
  starting transfers between devices  35.7 us (25%)
  waiting for transfers between devices  19.5 us (14%)
  local copies, waits for them, and re-layouts  11.9 us (8%)
  other arithmetic  5.9 us (4%)
  blocking collectives  4.62 us (3%)
    pallas_call x1, Pallas kernels, on_device(): pl.pallas_call(functools.partial(mesh_kernel, planes=planes, chunk=chunk,...  36.7 us
    ppermute x21, starting transfers between devices, passed_along(): return lax.ppermute(value, axis, pairs)  35.7 us
    pallas_call x4, Pallas kernels, on_device(): state, sent = step_call(place, state, beside, shown, near, bonds, rest)  25.4 us
    ppermute x21, waiting for transfers between devices, passed_along(): return lax.ppermute(value, axis, pairs)  19.5 us
    unnamed x45, local copies, waits for them, and re-layouts  7.84 us
  transfers between devices with their start and end apart: 21, of which 13 were waited for; matrix products, arithmetic and copies ran while one was open for 4% of the time, Pallas kernels for 0%

profile of v1, /device:TPU:1, one launch (start us, length us, event | category | flops | bytes accessed | tf_op | source)
XLA Modules:
  0.0 141.8 jit_solution(4521737604754004011)
XLA Ops:
  0.6 0.7 copy_bitcast_fusion.1
  1.4 1.3 pad_maximum_fusion.2.state_ref
  2.7 1.4 shard_map.184
  4.1 2.1 %collective-permute-start = (f32[4,128]{1,0:T(4,128)}, f32[4,128]{1,0:T(4,128)S(1)}, u32[]{:S(2)}, u32[]{:S(2)}) collective-permute-start(f32[4,128]{1,0:T(4,128)} %shard_map.184), channel_id=1, source_target_pairs={{0,4},{4,8},{8,12},{12,0},{1,5},{5,9},{9,13},{13,1},{2,6},{6,10},{... | collective-permute-start | bytes 6152 | tf_op jit(solution)/shard_map/ppermute | solution.py:253
  6.2 2.0 %collective-permute-start.1 = (f32[4,128]{1,0:T(4,128)}, f32[4,128]{1,0:T(4,128)S(1)}, u32[]{:S(2)}, u32[]{:S(2)}) collective-permute-start(f32[4,128]{1,0:T(4,128)} %shard_map.184), channel_id=1, source_target_pairs={{0,12},{4,0},{8,4},{12,8},{1,13},{5,1},{9,5},{13,9},{2,14},{6,2},{... | collective-permute-start | bytes 6152 | tf_op jit(solution)/shard_map/ppermute | solution.py:253
  8.2 2.5 %all-gather.2 = s32[2,34,512]{2,1,0:T(8,128)S(1)} all-gather(s32[1,34,512]{2,1,0:T(8,128)S(1)} %add_bitcast_fusion), channel_id=2, replica_groups=mesh['rep'=2,'tile'=4,'pen'=2,'sub'=2] {'sub'}, dimensions={0}, use_global_device_ids=true | all-gather | bytes 208896 | tf_op jit(solution)/shard_map/all_gather | solution.py:273
  10.8 0.6 pad_add_fusion.bonds_ref
  11.4 0.7 copy-done.6
  12.1 1.4 %collective-permute-start.2 = (f32[3,4,128]{2,1,0:T(4,128)S(1)}, f32[3,4,128]{2,1,0:T(4,128)S(1)}, u32[]{:S(2)}, u32[]{:S(2)}) collective-permute-start(f32[3,4,128]{2,1,0:T(4,128)S(1)} %pad_maximum_fusion.4), channel_id=1, source_target_pairs={{0,2},{2,0},{1,3},{3,1},{4,6},{6,4},{5,7},{7,5},{8,10},{10,8},{9,1... | collective-permute-start | bytes 18440 | tf_op jit(solution)/shard_map/ppermute | solution.py:253
  13.5 0.6 pad_add_fusion.1.place_ref
  14.2 0.6 slice.45
  14.9 2.1 %all-gather.1 = f32[1,1,4,512]{3,1,0,2:T(1,128)S(1)} all-gather(f32[1,1,2,512]{3,1,0,2:T(1,128)S(1)} %copy.23), channel_id=3, replica_groups=mesh['rep'=2,'tile'=4,'pen'=2,'sub'=2] {'sub'}, dimensions={2}, use_global_device_ids=true | all-gather | bytes 12288 | tf_op jit(solution)/shard_map/all_gather | solution.py:276
  17.0 0.6 concatenate.38.rest_ref
  18.2 6.3 %shard_map.185 = (f32[8,512]{1,0:T(8,128)}, f32[4,128]{1,0:T(4,128)}) custom-call(s32[2]{0:T(128)} %pad_add_fusion.1.place_ref, f32[8,512]{1,0:T(8,128)} %pad_maximum_fusion.2.state_ref, f32[9,4,128]{2,1,0:T(4,128)} %copy-done.1, s32[1,128]{1,0:T(1,128)} %bitcast.82, s32[64,512]{1,0:T(8,128)} %bitcast.70, s32[8,512]{1,0:T(8,128)} %pad_add_fusion.bonds_ref, ...), custom_call_target="tpu_custom_call" | custom-call | tf_op jit(solution)/shard_map/pallas_call | solution.py:303
  24.8 3.0 %collective-permute-start.4 = (f32[4,128]{1,0:T(4,128)}, f32[4,128]{1,0:T(4,128)S(1)}, u32[]{:S(2)}, u32[]{:S(2)}) collective-permute-start(f32[4,128]{1,0:T(4,128)} %get-tuple-element.11), channel_id=1, source_target_pairs={{0,12},{4,0},{8,4},{12,8},{1,13},{5,1},{9,5},{13,9},{2,14},{6,2},{... | collective-permute-start | bytes 6152 | tf_op jit(solution)/shard_map/ppermute | solution.py:253
  27.8 1.2 collective-permute-done.3
  29.0 0.7 copy-done.8
  29.7 2.4 %collective-permute-done.5 = f32[3,4,128]{2,1,0:T(4,128)S(1)} collective-permute-done((f32[3,4,128]{2,1,0:T(4,128)S(1)}, f32[3,4,128]{2,1,0:T(4,128)S(1)}, u32[]{:S(2)}, u32[]{:S(2)}) %collective-permute-start.5) | collective-permute-done | bytes 6176 | tf_op jit(solution)/shard_map/ppermute | solution.py:253
  32.8 6.3 %shard_map.186 = (f32[8,512]{1,0:T(8,128)}, f32[4,128]{1,0:T(4,128)}) custom-call(s32[2]{0:T(128)} %pad_add_fusion.1.place_ref, f32[8,512]{1,0:T(8,128)} %get-tuple-element.10.state_ref, f32[9,4,128]{2,1,0:T(4,128)} %copy-done.2, s32[1,128]{1,0:T(1,128)} %bitcast.83, s32[64,512]{1,0:T(8,128)} %bitcast.71, s32[8,512]{1,0:T(8,128)} %pad_add_fusion.bonds_ref, ...), custom_call_target="tpu_custom_call" | custom-call | tf_op jit(solution)/shard_map/pallas_call | solution.py:303
  39.2 3.2 %collective-permute-start.7 = (f32[4,128]{1,0:T(4,128)}, f32[4,128]{1,0:T(4,128)S(1)}, u32[]{:S(2)}, u32[]{:S(2)}) collective-permute-start(f32[4,128]{1,0:T(4,128)} %get-tuple-element.13), channel_id=1, source_target_pairs={{0,12},{4,0},{8,4},{12,8},{1,13},{5,1},{9,5},{13,9},{2,14},{6,2},{... | collective-permute-start | bytes 6152 | tf_op jit(solution)/shard_map/ppermute | solution.py:253
  42.4 1.2 collective-permute-done.6
  43.6 0.7 copy-done.9
  44.3 2.7 %collective-permute-done.8 = f32[3,4,128]{2,1,0:T(4,128)S(1)} collective-permute-done((f32[3,4,128]{2,1,0:T(4,128)S(1)}, f32[3,4,128]{2,1,0:T(4,128)S(1)}, u32[]{:S(2)}, u32[]{:S(2)}) %collective-permute-start.8) | collective-permute-done | bytes 6176 | tf_op jit(solution)/shard_map/ppermute | solution.py:253
  47.6 6.3 %shard_map.187 = (f32[8,512]{1,0:T(8,128)}, f32[4,128]{1,0:T(4,128)}) custom-call(s32[2]{0:T(128)} %pad_add_fusion.1.place_ref, f32[8,512]{1,0:T(8,128)} %get-tuple-element.12.state_ref, f32[9,4,128]{2,1,0:T(4,128)} %copy-done.3, s32[1,128]{1,0:T(1,128)} %bitcast.84, s32[64,512]{1,0:T(8,128)} %bitcast.72, s32[8,512]{1,0:T(8,128)} %pad_add_fusion.bonds_ref, ...), custom_call_target="tpu_custom_call" | custom-call | tf_op jit(solution)/shard_map/pallas_call | solution.py:303
  54.3 3.0 %collective-permute-start.10 = (f32[4,128]{1,0:T(4,128)}, f32[4,128]{1,0:T(4,128)S(1)}, u32[]{:S(2)}, u32[]{:S(2)}) collective-permute-start(f32[4,128]{1,0:T(4,128)} %get-tuple-element.15), channel_id=1, source_target_pairs={{0,12},{4,0},{8,4},{12,8},{1,13},{5,1},{9,5},{13,9},{2,14},{6,2},{... | collective-permute-start | bytes 6152 | tf_op jit(solution)/shard_map/ppermute | solution.py:253
  57.3 1.2 collective-permute-done.9
  58.5 0.7 copy-done.7
  59.2 0.6 copy-done.5
  59.9 1.8 %collective-permute-done.11 = f32[3,4,128]{2,1,0:T(4,128)S(1)} collective-permute-done((f32[3,4,128]{2,1,0:T(4,128)S(1)}, f32[3,4,128]{2,1,0:T(4,128)S(1)}, u32[]{:S(2)}, u32[]{:S(2)}) %collective-permute-start.11) | collective-permute-done | bytes 6176 | tf_op jit(solution)/shard_map/ppermute | solution.py:253
  62.3 6.3 %shard_map.188 = (f32[8,512]{1,0:T(8,128)}, f32[4,128]{1,0:T(4,128)}) custom-call(s32[2]{0:T(128)} %pad_add_fusion.1.place_ref, f32[8,512]{1,0:T(8,128)} %get-tuple-element.14.state_ref, f32[9,4,128]{2,1,0:T(4,128)} %copy-done.4, s32[1,128]{1,0:T(1,128)} %bitcast.85, s32[64,512]{1,0:T(8,128)} %bitcast.73, s32[8,512]{1,0:T(8,128)} %pad_add_fusion.bonds_ref, ...), custom_call_target="tpu_custom_call" | custom-call | tf_op jit(solution)/shard_map/pallas_call | solution.py:303
  68.6 0.8 add_subtract_fusion
  69.4 0.7 slice.38
  70.3 1.3 constant_dynamic-slice_fusion.1.mine_ref
  71.6 1.2 collective-permute-done.12
  72.8 0.6 collective-permute-start.13
  73.5 2.9 %collective-permute-start.14 = (f32[8,1024]{1,0:T(8,128)S(1)}, f32[8,1024]{1,0:T(8,128)S(1)}, u32[]{:S(2)}, u32[]{:S(2)}) collective-permute-start(f32[8,1024]{1,0:T(8,128)S(1)} %pad_maximum_fusion.1), channel_id=1, source_target_pairs={{0,8},{4,12},{8,0},{12,4},{1,9},{5,13},{9,1},{13,5},{2,10},{6,14},... | collective-permute-start | bytes 98312 | tf_op jit(solution)/shard_map/ppermute | solution.py:253
  77.8 1.4 collective-permute-done.15
  79.2 0.6 pad_maximum_fusion.atoms_ref
  79.8 36.7 %shard_map.189 = f32[4,1,1024]{2,1,0:T(1,128)} custom-call(s32[2]{0:T(128)} %pad_add_fusion.2.first_ref, f32[256]{0:T(256)} %constant.51.clone.lines_ref, f32[256]{0:T(256)} %constant.52.clone.squares_ref, f32[4,8,1024]{2,1,0:T(8,128)} %pad_maximum_fusion.atoms_ref, bf16[2,16,256]{2,1,0:T(8,128)(2,1)} %constant_dynamic-slice_fusion.1.mine_ref, ...), custom_call_target="tpu_custom_call" | custom-call | tf_op jit(solution)/shard_map/pallas_call | solution.py:320
  116.5 0.7 slice_bitcast_fusion.4
  117.2 2.4 %collective-permute-start.16 = (f32[1,1024]{1,0:T(1,128)S(1)}, f32[1,1024]{1,0:T(1,128)S(1)}, u32[]{:S(2)}, u32[]{:S(2)}) collective-permute-start(f32[1,1024]{1,0:T(1,128)S(1)} %get-tuple-element.23), channel_id=1, source_target_pairs={{0,12},{4,0},{8,4},{12,8},{1,13},{5,1},{9,5},{13,9},{2,14},{6,2},{... | collective-permute-start | bytes 12296 | tf_op jit(solution)/shard_map/ppermute | solution.py:253
  120.3 2.6 %collective-permute-done.17 = f32[1,1024]{1,0:T(1,128)S(1)} collective-permute-done((f32[1,1024]{1,0:T(1,128)S(1)}, f32[1,1024]{1,0:T(1,128)S(1)}, u32[]{:S(2)}, u32[]{:S(2)}) %collective-permute-start.17) | collective-permute-done | bytes 4128 | tf_op jit(solution)/shard_map/ppermute | solution.py:253
  122.9 0.9 collective-permute-done.18
  123.8 0.7 fusion.3
  124.8 2.2 %collective-permute-done.19 = f32[1,512]{1,0:T(1,128)S(1)} collective-permute-done((f32[1,512]{1,0:T(1,128)S(1)}, f32[1,512]{1,0:T(1,128)S(1)}, u32[]{:S(2)}, u32[]{:S(2)}) %collective-permute-start.19) | collective-permute-done | bytes 2080 | tf_op jit(solution)/shard_map/ppermute | solution.py:253
  127.0 13.0 %collective-permute-start.20 = (f32[1,256]{1,0:T(1,128)S(1)}, f32[1,256]{1,0:T(1,128)S(1)}, u32[]{:S(2)}, u32[]{:S(2)}) collective-permute-start(f32[1,256]{1,0:T(1,128)S(1)} %constant_dynamic-slice_fusion), channel_id=1, source_target_pairs={{0,1},{1,0},{2,3},{3,2},{4,5},{5,4},{6,7},{7,6},{8,9},{9,8},{10,11... | collective-permute-start | bytes 3080 | tf_op jit(solution)/shard_map/ppermute | solution.py:253
  140.0 0.6 copy.25
  140.6 0.6 copy.26
  (78 shorter events, 6.5 us)
Async XLA Ops:
  0.6 7.6 %copy-start = (s32[1,1,32,512]{3,2,1,0:T(8,128)S(1)}, s32[1,1,32,512]{3,2,1,0:T(8,128)}, u32[]{:S(2)}) copy-start(s32[1,1,32,512]{3,2,1,0:T(8,128)} %param.22) | copy-start | bytes 196612
  2.7 5.5 %copy-start.10 = (s32[1,1,2,512]{3,2,1,0:T(2,128)S(1)}, s32[1,1,2,512]{3,2,1,0:T(2,128)}, u32[]{:S(2)}) copy-start(s32[1,1,2,512]{3,2,1,0:T(2,128)} %param.23) | copy-start | bytes 12292
  4.1 7.3 %collective-permute-start = (f32[4,128]{1,0:T(4,128)}, f32[4,128]{1,0:T(4,128)S(1)}, u32[]{:S(2)}, u32[]{:S(2)}) collective-permute-start(f32[4,128]{1,0:T(4,128)} %shard_map.184), channel_id=1, source_target_pairs={{0,4},{4,8},{8,12},{12,0},{1,5},{5,9},{9,13},{13,1},{2,6},{6,10},{... | collective-permute-start | bytes 6152 | tf_op jit(solution)/shard_map/ppermute | solution.py:253
  6.2 5.2 %collective-permute-start.1 = (f32[4,128]{1,0:T(4,128)}, f32[4,128]{1,0:T(4,128)S(1)}, u32[]{:S(2)}, u32[]{:S(2)}) collective-permute-start(f32[4,128]{1,0:T(4,128)} %shard_map.184), channel_id=1, source_target_pairs={{0,12},{4,0},{8,4},{12,8},{1,13},{5,1},{9,5},{13,9},{2,14},{6,2},{... | collective-permute-start | bytes 6152 | tf_op jit(solution)/shard_map/ppermute | solution.py:253
  11.4 0.7 copy-start.6
  12.1 5.5 %collective-permute-start.2 = (f32[3,4,128]{2,1,0:T(4,128)S(1)}, f32[3,4,128]{2,1,0:T(4,128)S(1)}, u32[]{:S(2)}, u32[]{:S(2)}) collective-permute-start(f32[3,4,128]{2,1,0:T(4,128)S(1)} %pad_maximum_fusion.4), channel_id=1, source_target_pairs={{0,2},{2,0},{1,3},{3,1},{4,6},{6,4},{5,7},{7,5},{8,10},{10,8},{9,1... | collective-permute-start | bytes 18440 | tf_op jit(solution)/shard_map/ppermute | solution.py:253
  14.2 0.7 copy-start.11
  17.6 0.6 copy-start.1
  24.6 4.4 %collective-permute-start.3 = (f32[4,128]{1,0:T(4,128)}, f32[4,128]{1,0:T(4,128)S(1)}, u32[]{:S(2)}, u32[]{:S(2)}) collective-permute-start(f32[4,128]{1,0:T(4,128)} %get-tuple-element.11), channel_id=1, source_target_pairs={{0,4},{4,8},{8,12},{12,0},{1,5},{5,9},{9,13},{13,1},{2,6},{6,10},{... | collective-permute-start | bytes 6152 | tf_op jit(solution)/shard_map/ppermute | solution.py:253
  24.8 4.2 %collective-permute-start.4 = (f32[4,128]{1,0:T(4,128)}, f32[4,128]{1,0:T(4,128)S(1)}, u32[]{:S(2)}, u32[]{:S(2)}) collective-permute-start(f32[4,128]{1,0:T(4,128)} %get-tuple-element.11), channel_id=1, source_target_pairs={{0,12},{4,0},{8,4},{12,8},{1,13},{5,1},{9,5},{13,9},{2,14},{6,2},{... | collective-permute-start | bytes 6152 | tf_op jit(solution)/shard_map/ppermute | solution.py:253
  29.0 0.7 copy-start.8
  29.7 2.5 %collective-permute-start.5 = (f32[3,4,128]{2,1,0:T(4,128)S(1)}, f32[3,4,128]{2,1,0:T(4,128)S(1)}, u32[]{:S(2)}, u32[]{:S(2)}) collective-permute-start(f32[3,4,128]{2,1,0:T(4,128)S(1)} %pad_maximum_fusion.5), channel_id=1, source_target_pairs={{0,2},{2,0},{1,3},{3,1},{4,6},{6,4},{5,7},{7,5},{8,10},{10,8},{9,1... | collective-permute-start | bytes 18440 | tf_op jit(solution)/shard_map/ppermute | solution.py:253
  32.2 0.6 copy-start.2
  39.1 4.4 %collective-permute-start.6 = (f32[4,128]{1,0:T(4,128)}, f32[4,128]{1,0:T(4,128)S(1)}, u32[]{:S(2)}, u32[]{:S(2)}) collective-permute-start(f32[4,128]{1,0:T(4,128)} %get-tuple-element.13), channel_id=1, source_target_pairs={{0,4},{4,8},{8,12},{12,0},{1,5},{5,9},{9,13},{13,1},{2,6},{6,10},{... | collective-permute-start | bytes 6152 | tf_op jit(solution)/shard_map/ppermute | solution.py:253
  39.2 4.4 %collective-permute-start.7 = (f32[4,128]{1,0:T(4,128)}, f32[4,128]{1,0:T(4,128)S(1)}, u32[]{:S(2)}, u32[]{:S(2)}) collective-permute-start(f32[4,128]{1,0:T(4,128)} %get-tuple-element.13), channel_id=1, source_target_pairs={{0,12},{4,0},{8,4},{12,8},{1,13},{5,1},{9,5},{13,9},{2,14},{6,2},{... | collective-permute-start | bytes 6152 | tf_op jit(solution)/shard_map/ppermute | solution.py:253
  43.6 0.7 copy-start.9
  44.3 2.7 %collective-permute-start.8 = (f32[3,4,128]{2,1,0:T(4,128)S(1)}, f32[3,4,128]{2,1,0:T(4,128)S(1)}, u32[]{:S(2)}, u32[]{:S(2)}) collective-permute-start(f32[3,4,128]{2,1,0:T(4,128)S(1)} %pad_maximum_fusion.6), channel_id=1, source_target_pairs={{0,2},{2,0},{1,3},{3,1},{4,6},{6,4},{5,7},{7,5},{8,10},{10,8},{9,1... | collective-permute-start | bytes 18440 | tf_op jit(solution)/shard_map/ppermute | solution.py:253
  47.0 0.6 copy-start.3
  54.0 4.5 %collective-permute-start.9 = (f32[4,128]{1,0:T(4,128)}, f32[4,128]{1,0:T(4,128)S(1)}, u32[]{:S(2)}, u32[]{:S(2)}) collective-permute-start(f32[4,128]{1,0:T(4,128)} %get-tuple-element.15), channel_id=1, source_target_pairs={{0,4},{4,8},{8,12},{12,0},{1,5},{5,9},{9,13},{13,1},{2,6},{6,10},{... | collective-permute-start | bytes 6152 | tf_op jit(solution)/shard_map/ppermute | solution.py:253
  54.3 4.1 %collective-permute-start.10 = (f32[4,128]{1,0:T(4,128)}, f32[4,128]{1,0:T(4,128)S(1)}, u32[]{:S(2)}, u32[]{:S(2)}) collective-permute-start(f32[4,128]{1,0:T(4,128)} %get-tuple-element.15), channel_id=1, source_target_pairs={{0,12},{4,0},{8,4},{12,8},{1,13},{5,1},{9,5},{13,9},{2,14},{6,2},{... | collective-permute-start | bytes 6152 | tf_op jit(solution)/shard_map/ppermute | solution.py:253
  58.5 0.7 copy-start.7
  59.2 0.7 copy-start.5
  59.2 2.5 %collective-permute-start.11 = (f32[3,4,128]{2,1,0:T(4,128)S(1)}, f32[3,4,128]{2,1,0:T(4,128)S(1)}, u32[]{:S(2)}, u32[]{:S(2)}) collective-permute-start(f32[3,4,128]{2,1,0:T(4,128)S(1)} %pad_maximum_fusion.7), channel_id=1, source_target_pairs={{0,2},{2,0},{1,3},{3,1},{4,6},{6,4},{5,7},{7,5},{8,10},{10,8},{9,1... | collective-permute-start | bytes 18440 | tf_op jit(solution)/shard_map/ppermute | solution.py:253
  61.7 0.6 copy-start.4
  70.2 2.7 %collective-permute-start.12 = (f32[8,512]{1,0:T(8,128)S(1)}, f32[8,512]{1,0:T(8,128)S(1)}, u32[]{:S(2)}, u32[]{:S(2)}) collective-permute-start(f32[8,512]{1,0:T(8,128)S(1)} %pad_maximum_fusion.3), channel_id=1, source_target_pairs={{0,2},{2,0},{1,3},{3,1},{4,6},{6,4},{5,7},{7,5},{8,10},{10,8},{9,1... | collective-permute-start | bytes 49160 | tf_op jit(solution)/shard_map/ppermute | solution.py:253
  72.8 4.7 %collective-permute-start.13 = (f32[8,1024]{1,0:T(8,128)S(1)}, f32[8,1024]{1,0:T(8,128)S(1)}, u32[]{:S(2)}, u32[]{:S(2)}) collective-permute-start(f32[8,1024]{1,0:T(8,128)S(1)} %pad_maximum_fusion.1), channel_id=1, source_target_pairs={{0,4},{4,8},{8,12},{12,0},{1,5},{5,9},{9,13},{13,1},{2,6},{6,10},{... | collective-permute-start | bytes 98312 | tf_op jit(solution)/shard_map/ppermute | solution.py:253
  73.5 4.3 %collective-permute-start.14 = (f32[8,1024]{1,0:T(8,128)S(1)}, f32[8,1024]{1,0:T(8,128)S(1)}, u32[]{:S(2)}, u32[]{:S(2)}) collective-permute-start(f32[8,1024]{1,0:T(8,128)S(1)} %pad_maximum_fusion.1), channel_id=1, source_target_pairs={{0,8},{4,12},{8,0},{12,4},{1,9},{5,13},{9,1},{13,5},{2,10},{6,14},... | collective-permute-start | bytes 98312 | tf_op jit(solution)/shard_map/ppermute | solution.py:253
  76.4 2.8 %collective-permute-start.15 = (f32[8,1024]{1,0:T(8,128)S(1)}, f32[8,1024]{1,0:T(8,128)S(1)}, u32[]{:S(2)}, u32[]{:S(2)}) collective-permute-start(f32[8,1024]{1,0:T(8,128)S(1)} %pad_maximum_fusion.1), channel_id=1, source_target_pairs={{0,12},{4,0},{8,4},{12,8},{1,13},{5,1},{9,5},{13,9},{2,14},{6,2},{... | collective-permute-start | bytes 98312 | tf_op jit(solution)/shard_map/ppermute | solution.py:253
  117.2 3.1 %collective-permute-start.16 = (f32[1,1024]{1,0:T(1,128)S(1)}, f32[1,1024]{1,0:T(1,128)S(1)}, u32[]{:S(2)}, u32[]{:S(2)}) collective-permute-start(f32[1,1024]{1,0:T(1,128)S(1)} %get-tuple-element.23), channel_id=1, source_target_pairs={{0,12},{4,0},{8,4},{12,8},{1,13},{5,1},{9,5},{13,9},{2,14},{6,2},{... | collective-permute-start | bytes 12296 | tf_op jit(solution)/shard_map/ppermute | solution.py:253
  119.6 3.4 %collective-permute-start.17 = (f32[1,1024]{1,0:T(1,128)S(1)}, f32[1,1024]{1,0:T(1,128)S(1)}, u32[]{:S(2)}, u32[]{:S(2)}) collective-permute-start(f32[1,1024]{1,0:T(1,128)S(1)} %get-tuple-element.25), channel_id=1, source_target_pairs={{0,8},{4,12},{8,0},{12,4},{1,9},{5,13},{9,1},{13,5},{2,10},{6,14},... | collective-permute-start | bytes 12296 | tf_op jit(solution)/shard_map/ppermute | solution.py:253
  119.6 4.3 %collective-permute-start.18 = (f32[1,1024]{1,0:T(1,128)S(1)}, f32[1,1024]{1,0:T(1,128)S(1)}, u32[]{:S(2)}, u32[]{:S(2)}) collective-permute-start(f32[1,1024]{1,0:T(1,128)S(1)} %get-tuple-element.24), channel_id=1, source_target_pairs={{0,4},{4,8},{8,12},{12,0},{1,5},{5,9},{9,13},{13,1},{2,6},{6,10},{... | collective-permute-start | bytes 12296 | tf_op jit(solution)/shard_map/ppermute | solution.py:253
  124.5 2.5 %collective-permute-start.19 = (f32[1,512]{1,0:T(1,128)S(1)}, f32[1,512]{1,0:T(1,128)S(1)}, u32[]{:S(2)}, u32[]{:S(2)}) collective-permute-start(f32[1,512]{1,0:T(1,128)S(1)} %slice.52), channel_id=1, source_target_pairs={{0,2},{2,0},{1,3},{3,1},{4,6},{6,4},{5,7},{7,5},{8,10},{10,8},{9,1... | collective-permute-start | bytes 6152 | tf_op jit(solution)/shard_map/ppermute | solution.py:253
  127.0 14.2 %collective-permute-start.20 = (f32[1,256]{1,0:T(1,128)S(1)}, f32[1,256]{1,0:T(1,128)S(1)}, u32[]{:S(2)}, u32[]{:S(2)}) collective-permute-start(f32[1,256]{1,0:T(1,128)S(1)} %constant_dynamic-slice_fusion), channel_id=1, source_target_pairs={{0,1},{1,0},{2,3},{3,2},{4,5},{5,4},{6,7},{7,6},{8,9},{9,8},{10,11... | collective-permute-start | bytes 3080 | tf_op jit(solution)/shard_map/ppermute | solution.py:253

commit v2 on v1

--- a/solution.py
+++ b/solution.py
@@ -38,24 +38,66 @@
     return total[:4]
 
 
-def export_kernel(state_ref, shown_ref, sent_ref):
-    sent_ref[...] = shown_rows(state_ref[...], shown_ref[...])
-
-
-def step_kernel(
-    place_ref, state_ref, beside_ref, shown_ref, partners_ref, bonds_ref, rest_ref,
-    out_ref, sent_ref, table, *, tile_count, pen_count,
+def dynamics_kernel(
+    state_ref, shown_ref, partners_ref, bonds_ref, rest_ref,
+    out_ref, table, sent, beside, send_sem, recv_sem, *, tile_count, pen_count,
 ):
+    tile_index, pen_index = lax.axis_index("tile"), lax.axis_index("pen")
+    around = [(i, j) for i in range(3) for j in range(3) if (i, j) != (1, 1)]
+
+    def neighbour(i, j):
+        return {
+            "tile": lax.rem(tile_index + (i - 1) + tile_count, tile_count),
+            "pen": lax.rem(pen_index + (j - 1) + pen_count, pen_count),
+        }
+
+    barrier = pltpu.get_barrier_semaphore()
+    for i, j in around:
+        pl.semaphore_signal(
+            barrier, inc=1, device_id=neighbour(i, j), device_id_type=pl.DeviceIdType.MESH
+        )
+    pl.semaphore_wait(barrier, len(around))
+    out_ref[...] = state_ref[...]
+
+    def step(n, carry):
+        sent[n] = shown_rows(out_ref[...], shown_ref[...])
+        copies = []
+        for place, (i, j) in enumerate(around):
+            copy = pltpu.make_async_remote_copy(
+                src_ref=sent.at[n],
+                dst_ref=beside.at[n, len(around) - 1 - place],
+                send_sem=send_sem.at[n, place],
+                recv_sem=recv_sem.at[n, len(around) - 1 - place],
+                device_id=neighbour(i, j),
+                device_id_type=pl.DeviceIdType.MESH,
+            )
+            copy.start()
+            copies.append(copy)
+        one_step(
+            tile_index, pen_index, tile_count, pen_count, n, copies, around,
+            out_ref, beside, partners_ref, bonds_ref, rest_ref, table,
+        )
+        return carry
+
+    lax.fori_loop(0, INNER, step, 0)
+
+
+def one_step(
+    tile_index, pen_index, tile_count, pen_count, n, copies, around,
+    state_ref, beside_ref, partners_ref, bonds_ref, rest_ref, table,
+):
+    out_ref = state_ref
     atoms = state_ref.shape[1]
     own_blocks = atoms // LANES
-    halo_blocks = beside_ref.shape[2] // LANES
-    tile_index, pen_index = place_ref[0], place_ref[1]
+    halo_blocks = beside_ref.shape[3] // LANES
     blocks = list(range(own_blocks))
     for block in range(own_blocks):
         for row in range(4):
             table[block * 4 + row] = jnp.broadcast_to(
                 state_ref[row : row + 1, block * LANES : (block + 1) * LANES], (8, LANES)
             )
+    for copy in copies:
+        copy.wait()
     for i in range(3):
         near_x = tile_index + (i - 1)
         move_x = jnp.where(near_x < 0, -float(GRID), jnp.where(near_x >= tile_count, float(GRID), 0.0))
@@ -64,7 +106,7 @@
                 continue
             near_y = pen_index + (j - 1)
             move_y = jnp.where(near_y < 0, -float(GRID), jnp.where(near_y >= pen_count, float(GRID), 0.0))
-            patch = beside_ref[j * 3 + i]
+            patch = beside_ref[n, around.index((i, j))]
             for part in range(halo_blocks):
                 block = own_blocks + (i * 3 + j) * halo_blocks + part
                 blocks.append(block)
@@ -119,7 +161,6 @@
             out_ref[r : r + 1, lanes] = state_ref[r : r + 1, lanes] + time_step * speed
         out_ref[3:4, lanes] = state_ref[3:4, lanes]
         out_ref[7:8, lanes] = scale
-    sent_ref[...] = shown_rows(out_ref[...], shown_ref[...])
 
 
 def split(value):
@@ -265,7 +306,6 @@
     atoms = positions.shape[3]
     exported = export_rows.shape[2]
     planes = GRID // tile_count
-    place = jnp.stack([tile_index, pen_index]).astype(jnp.int32)
     state = jnp.concatenate(
         [positions[:, 0, 0], charges[0], velocities[:, 0, 0], inverse_mass[0]], axis=0
     )
@@ -283,24 +323,21 @@
     rest = jnp.concatenate([rest, jnp.ones((fill, atoms), f32)], axis=0)
     vmem = pl.BlockSpec(memory_space=pltpu.VMEM)
     smem = pl.BlockSpec(memory_space=pltpu.SMEM)
-    sent_shape = jax.ShapeDtypeStruct((4, exported), f32)
-    sent = pl.pallas_call(
-        export_kernel, out_shape=sent_shape, in_specs=[vmem, vmem], out_specs=vmem
-    )(state, shown)
     columns = (atoms + 9 * exported) // LANES
-    step_call = pl.pallas_call(
-        functools.partial(step_kernel, tile_count=tile_count, pen_count=pen_count),
-        out_shape=(jax.ShapeDtypeStruct(state.shape, f32), sent_shape),
-        in_specs=[smem] + [vmem] * 6,
-        out_specs=(vmem, vmem),
-        scratch_shapes=[pltpu.VMEM((columns * 4, 8, LANES), f32)],
-    )
-    for step in range(INNER):
-        column = jnp.stack([passed_along(sent, "tile", 1), sent, passed_along(sent, "tile", -1)])
-        low = passed_along(column, "pen", 1)
-        high = low if pen_count == 2 else passed_along(column, "pen", -1)
-        beside = jnp.concatenate([low, column, high], axis=0)
-        state, sent = step_call(place, state, beside, shown, near, bonds, rest)
+    state = pl.pallas_call(
+        functools.partial(dynamics_kernel, tile_count=tile_count, pen_count=pen_count),
+        out_shape=jax.ShapeDtypeStruct(state.shape, f32),
+        in_specs=[vmem] * 5,
+        out_specs=vmem,
+        scratch_shapes=[
+            pltpu.VMEM((columns * 4, 8, LANES), f32),
+            pltpu.VMEM((INNER, 4, exported), f32),
+            pltpu.VMEM((INNER, 8, 4, exported), f32),
+            pltpu.SemaphoreType.DMA((INNER, 8)),
+            pltpu.SemaphoreType.DMA((INNER, 8)),
+        ],
+        compiler_params=pltpu.CompilerParams(collective_id=0, has_side_effects=True),
+    )(state, shown, near, bonds, rest)
     coords, speeds = state[0:3], state[4:7]
     offsets = block_offsets[:, 0, 0].astype(f32)
     packed = jnp.concatenate([coords - (offsets + 1.0), offsets, state[3:4], state[3:4]], axis=0)

time: 143 us -> 119 us (0.83)
  starting transfers between devices: 35.7 us -> 16.7 us
  Pallas kernels: 63.4 us -> 76.1 us
  waiting for transfers between devices: 19.5 us -> 8.22 us
  local copies, waits for them, and re-layouts: 11.9 us -> 7.3 us
    ppermute x21 -> x9, starting transfers between devices: 35.7 us -> 16.7 us  [passed_along(): return lax.ppermute(value, axis, pairs)]
    pallas_call x5 -> x1, Pallas kernels: 26.7 us -> 39.4 us  [on_device(): pl.pallas_call(functools.partial(dynamics_kernel, tile_count=tile_count,...]
    ppermute x21 -> x9, waiting for transfers between devices: 19.5 us -> 8.22 us  [passed_along(): return lax.ppermute(value, axis, pairs)]
    unnamed x45 -> x17, local copies, waits for them, and re-layouts: 7.84 us -> 3.27 us
  transfers between devices with their start and end apart: 21 -> 9, of which waited for: 13 -> 7; matrix products, arithmetic and copies ran while one was open for 4% -> 3% of each run, Pallas kernels for 0% -> 0%
where the time goes in v2:
time: 119 us; the launch traced here: 118 us
  Pallas kernels  76.1 us (64%)
  starting transfers between devices  16.7 us (14%)
  waiting for transfers between devices  8.22 us (7%)
  local copies, waits for them, and re-layouts  7.3 us (6%)
  other arithmetic  5.42 us (5%)
  blocking collectives  3.71 us (3%)
    pallas_call x1, Pallas kernels, on_device(): pl.pallas_call(functools.partial(dynamics_kernel, tile_count=tile_count,...  39.4 us
    pallas_call x1, Pallas kernels, on_device(): pl.pallas_call(functools.partial(mesh_kernel, planes=planes, chunk=chunk,...  36.7 us
    ppermute x9, starting transfers between devices, passed_along(): return lax.ppermute(value, axis, pairs)  16.7 us
    ppermute x9, waiting for transfers between devices, passed_along(): return lax.ppermute(value, axis, pairs)  8.22 us
    unnamed x17, local copies, waits for them, and re-layouts  3.27 us
  transfers between devices with their start and end apart: 9, of which 7 were waited for; matrix products, arithmetic and copies ran while one was open for 3% of the time, Pallas kernels for 0%

profile of v2, /device:TPU:1, one launch (start us, length us, event | category | flops | bytes accessed | tf_op | source)
XLA Modules:
  0.0 118.1 jit_solution(5910718495609777927)
XLA Ops:
  0.6 0.9 add_bitcast_fusion
  1.5 1.9 %all-gather.2 = s32[2,34,512]{2,1,0:T(8,128)S(1)} all-gather(s32[1,34,512]{2,1,0:T(8,128)S(1)} %add_bitcast_fusion), channel_id=2, replica_groups=mesh['rep'=2,'tile'=4,'pen'=2,'sub'=2] {'sub'}, dimensions={0}, use_global_device_ids=true | all-gather | bytes 208896 | tf_op jit(solution)/shard_map/all_gather | solution.py:313
  3.4 0.7 slice.45
  4.1 0.0 copy-start.3
  4.1 0.7 copy-done.3
  4.8 1.8 %all-gather.1 = f32[1,1,4,512]{3,1,0,2:T(1,128)S(1)} all-gather(f32[1,1,2,512]{3,1,0,2:T(1,128)S(1)} %copy.23), channel_id=3, replica_groups=mesh['rep'=2,'tile'=4,'pen'=2,'sub'=2] {'sub'}, dimensions={2}, use_global_device_ids=true | all-gather | bytes 12288 | tf_op jit(solution)/shard_map/all_gather | solution.py:316
  6.6 0.0 copy-start.1
  6.6 0.0 copy-start.2
  6.6 0.7 copy-done.1
  7.3 0.0 copy-done.2
  7.3 0.6 pad_add_fusion.bonds_ref
  7.9 0.6 concatenate.21.rest_ref
  8.5 0.0 copy-start.5
  8.5 0.0 copy-start.4
  8.5 0.7 copy-done.5
  9.2 0.0 copy-done.4
  9.2 0.6 pad_maximum_fusion.2.state_ref
  9.8 39.4 %shard_map.184 = f32[8,512]{1,0:T(8,128)} custom-call(f32[8,512]{1,0:T(8,128)} %pad_maximum_fusion.2.state_ref, s32[1,128]{1,0:T(1,128)} %bitcast.55, s32[64,512]{1,0:T(8,128)} %bitcast.45, s32[8,512]{1,0:T(8,128)} %pad_add_fusion.bonds_ref, f32[8,512]{1,0:T(8,128)} %concatenate.21.rest_ref), custom_call_target="tpu_custom_call" | custom-call | tf_op jit(solution)/shard_map/pallas_call | solution.py:327
  49.2 0.7 slice.38
  50.0 0.0 copy-done
  50.0 0.8 add_subtract_fusion
  50.8 0.3 collective-permute-start
  51.1 1.3 %constant_dynamic-slice_fusion.1.mine_ref = bf16[2,16,256]{2,1,0:T(8,128)(2,1)} fusion(bf16[2,256,256]{2,1,0:T(8,128)(2,1)} %constant.75.cas_ref, s32[]{:T(128)S(6)} %select_n.16), kind=kLoop, calls=%fused_computation.24 | loop fusion | bytes 32772 | tf_op jit(solution)/shard_map/dynamic_slice | solution.py:371
  52.5 1.0 collective-permute-done
  53.5 0.1 collective-permute-start.1
  53.5 0.8 collective-permute-start.2
  54.3 2.5 %collective-permute-start.3 = (f32[8,1024]{1,0:T(8,128)S(1)}, f32[8,1024]{1,0:T(8,128)S(1)}, u32[]{:S(2)}, u32[]{:S(2)}) collective-permute-start(f32[8,1024]{1,0:T(8,128)S(1)} %pad_maximum_fusion.1), channel_id=1, source_target_pairs={{0,12},{4,0},{8,4},{12,8},{1,13},{5,1},{9,5},{13,9},{2,14},{6,2},{... | collective-permute-start | bytes 98312 | tf_op jit(solution)/shard_map/ppermute | solution.py:294
  56.8 0.6 pad_add_fusion.1.first_ref
  57.4 0.7 collective-permute-done.1
  58.1 0.0 collective-permute-done.2
  58.1 0.3 collective-permute-done.3
  58.4 0.7 pad_maximum_fusion.atoms_ref
  59.1 36.7 %shard_map.185 = f32[4,1,1024]{2,1,0:T(1,128)} custom-call(s32[2]{0:T(128)} %pad_add_fusion.1.first_ref, f32[256]{0:T(256)} %constant.51.clone.lines_ref, f32[256]{0:T(256)} %constant.52.clone.squares_ref, f32[4,8,1024]{2,1,0:T(8,128)} %pad_maximum_fusion.atoms_ref, bf16[2,16,256]{2,1,0:T(8,128)(2,1)} %constant_dynamic-slice_fusion.1.mine_ref, ...), custom_call_target="tpu_custom_call" | custom-call | tf_op jit(solution)/shard_map/pallas_call | solution.py:357
  95.8 0.7 slice_bitcast_fusion.4
  96.5 2.9 %collective-permute-start.4 = (f32[1,1024]{1,0:T(1,128)S(1)}, f32[1,1024]{1,0:T(1,128)S(1)}, u32[]{:S(2)}, u32[]{:S(2)}) collective-permute-start(f32[1,1024]{1,0:T(1,128)S(1)} %get-tuple-element.9), channel_id=1, source_target_pairs={{0,12},{4,0},{8,4},{12,8},{1,13},{5,1},{9,5},{13,9},{2,14},{6,2},{... | collective-permute-start | bytes 12296 | tf_op jit(solution)/shard_map/ppermute | solution.py:294
  99.4 0.0 collective-permute-start.5
  99.4 0.3 collective-permute-start.6
  99.7 0.5 collective-permute-done.4
  100.1 2.6 %collective-permute-done.5 = f32[1,1024]{1,0:T(1,128)S(1)} collective-permute-done((f32[1,1024]{1,0:T(1,128)S(1)}, f32[1,1024]{1,0:T(1,128)S(1)}, u32[]{:S(2)}, u32[]{:S(2)}) %collective-permute-start.5) | collective-permute-done | bytes 4128 | tf_op jit(solution)/shard_map/ppermute | solution.py:294
  102.7 0.9 collective-permute-done.6
  103.6 0.7 fusion.3
  104.4 0.3 collective-permute-start.7
  104.7 2.2 %collective-permute-done.7 = f32[1,512]{1,0:T(1,128)S(1)} collective-permute-done((f32[1,512]{1,0:T(1,128)S(1)}, f32[1,512]{1,0:T(1,128)S(1)}, u32[]{:S(2)}, u32[]{:S(2)}) %collective-permute-start.7) | collective-permute-done | bytes 2080 | tf_op jit(solution)/shard_map/ppermute | solution.py:294
  106.9 9.5 %collective-permute-start.8 = (f32[1,256]{1,0:T(1,128)S(1)}, f32[1,256]{1,0:T(1,128)S(1)}, u32[]{:S(2)}, u32[]{:S(2)}) collective-permute-start(f32[1,256]{1,0:T(1,128)S(1)} %constant_dynamic-slice_fusion), channel_id=1, source_target_pairs={{0,1},{1,0},{2,3},{3,2},{4,5},{5,4},{6,7},{7,6},{8,9},{9,8},{10,11... | collective-permute-start | bytes 3080 | tf_op jit(solution)/shard_map/ppermute | solution.py:294
  116.3 0.6 copy.25
  116.9 0.6 copy.26
  117.5 0.0 collective-permute-done.8
  117.5 0.6 add_bitcast_fusion.1
  (13 shorter events, 0.1 us)
Async XLA Ops:
  4.1 0.7 copy-start.3
  6.6 0.7 copy-start.1
  6.6 0.7 copy-start.2
  8.5 0.7 copy-start.5
  8.5 0.7 copy-start.4
  9.8 40.2 %copy-start = (s32[3,1,1,512]{3,2,1,0:T(1,128)S(1)}, s32[3,1,1,512]{3,2,1,0:T(1,128)}, u32[]{:S(2)}) copy-start(s32[3,1,1,512]{3,2,1,0:T(1,128)} %param.25) | copy-start | bytes 18436
  50.8 2.7 %collective-permute-start = (f32[8,512]{1,0:T(8,128)S(1)}, f32[8,512]{1,0:T(8,128)S(1)}, u32[]{:S(2)}, u32[]{:S(2)}) collective-permute-start(f32[8,512]{1,0:T(8,128)S(1)} %pad_maximum_fusion.3), channel_id=1, source_target_pairs={{0,2},{2,0},{1,3},{3,1},{4,6},{6,4},{5,7},{7,5},{8,10},{10,8},{9,1... | collective-permute-start | bytes 49160 | tf_op jit(solution)/shard_map/ppermute | solution.py:294
  53.5 4.6 %collective-permute-start.1 = (f32[8,1024]{1,0:T(8,128)S(1)}, f32[8,1024]{1,0:T(8,128)S(1)}, u32[]{:S(2)}, u32[]{:S(2)}) collective-permute-start(f32[8,1024]{1,0:T(8,128)S(1)} %pad_maximum_fusion.1), channel_id=1, source_target_pairs={{0,4},{4,8},{8,12},{12,0},{1,5},{5,9},{9,13},{13,1},{2,6},{6,10},{... | collective-permute-start | bytes 98312 | tf_op jit(solution)/shard_map/ppermute | solution.py:294
  53.5 4.6 %collective-permute-start.2 = (f32[8,1024]{1,0:T(8,128)S(1)}, f32[8,1024]{1,0:T(8,128)S(1)}, u32[]{:S(2)}, u32[]{:S(2)}) collective-permute-start(f32[8,1024]{1,0:T(8,128)S(1)} %pad_maximum_fusion.1), channel_id=1, source_target_pairs={{0,8},{4,12},{8,0},{12,4},{1,9},{5,13},{9,1},{13,5},{2,10},{6,14},... | collective-permute-start | bytes 98312 | tf_op jit(solution)/shard_map/ppermute | solution.py:294
  54.3 4.1 %collective-permute-start.3 = (f32[8,1024]{1,0:T(8,128)S(1)}, f32[8,1024]{1,0:T(8,128)S(1)}, u32[]{:S(2)}, u32[]{:S(2)}) collective-permute-start(f32[8,1024]{1,0:T(8,128)S(1)} %pad_maximum_fusion.1), channel_id=1, source_target_pairs={{0,12},{4,0},{8,4},{12,8},{1,13},{5,1},{9,5},{13,9},{2,14},{6,2},{... | collective-permute-start | bytes 98312 | tf_op jit(solution)/shard_map/ppermute | solution.py:294
  96.5 3.7 %collective-permute-start.4 = (f32[1,1024]{1,0:T(1,128)S(1)}, f32[1,1024]{1,0:T(1,128)S(1)}, u32[]{:S(2)}, u32[]{:S(2)}) collective-permute-start(f32[1,1024]{1,0:T(1,128)S(1)} %get-tuple-element.9), channel_id=1, source_target_pairs={{0,12},{4,0},{8,4},{12,8},{1,13},{5,1},{9,5},{13,9},{2,14},{6,2},{... | collective-permute-start | bytes 12296 | tf_op jit(solution)/shard_map/ppermute | solution.py:294
  99.4 3.4 %collective-permute-start.5 = (f32[1,1024]{1,0:T(1,128)S(1)}, f32[1,1024]{1,0:T(1,128)S(1)}, u32[]{:S(2)}, u32[]{:S(2)}) collective-permute-start(f32[1,1024]{1,0:T(1,128)S(1)} %get-tuple-element.11), channel_id=1, source_target_pairs={{0,8},{4,12},{8,0},{12,4},{1,9},{5,13},{9,1},{13,5},{2,10},{6,14},... | collective-permute-start | bytes 12296 | tf_op jit(solution)/shard_map/ppermute | solution.py:294
  99.4 4.3 %collective-permute-start.6 = (f32[1,1024]{1,0:T(1,128)S(1)}, f32[1,1024]{1,0:T(1,128)S(1)}, u32[]{:S(2)}, u32[]{:S(2)}) collective-permute-start(f32[1,1024]{1,0:T(1,128)S(1)} %get-tuple-element.10), channel_id=1, source_target_pairs={{0,4},{4,8},{8,12},{12,0},{1,5},{5,9},{9,13},{13,1},{2,6},{6,10},{... | collective-permute-start | bytes 12296 | tf_op jit(solution)/shard_map/ppermute | solution.py:294
  104.4 2.5 %collective-permute-start.7 = (f32[1,512]{1,0:T(1,128)S(1)}, f32[1,512]{1,0:T(1,128)S(1)}, u32[]{:S(2)}, u32[]{:S(2)}) collective-permute-start(f32[1,512]{1,0:T(1,128)S(1)} %slice.52), channel_id=1, source_target_pairs={{0,2},{2,0},{1,3},{3,1},{4,6},{6,4},{5,7},{7,5},{8,10},{10,8},{9,1... | collective-permute-start | bytes 6152 | tf_op jit(solution)/shard_map/ppermute | solution.py:294
  106.9 10.7 %collective-permute-start.8 = (f32[1,256]{1,0:T(1,128)S(1)}, f32[1,256]{1,0:T(1,128)S(1)}, u32[]{:S(2)}, u32[]{:S(2)}) collective-permute-start(f32[1,256]{1,0:T(1,128)S(1)} %constant_dynamic-slice_fusion), channel_id=1, source_target_pairs={{0,1},{1,0},{2,3},{3,2},{4,5},{5,4},{6,7},{7,6},{8,9},{9,8},{10,11... | collective-permute-start | bytes 3080 | tf_op jit(solution)/shard_map/ppermute | solution.py:294
